TPU v7x, 32 devices: a whole 2x2x4 slice. The times are simulated.
32 devices in a mesh: dp: 4 (over y, core), expert: 4 (over z), tensor: 2 (over x).
Axes of the slice: x: 2, y: 2, z: 4, core: 2. Of those that a mesh axis runs over, the one named last changes fastest.
Arguments:
- router_input: bfloat16 [1024, 2048], P(('dp', 'expert'), 'tensor'), may hold values from -6 to 6
- router_weight: bfloat16 [2048, 8], replicated, may hold values from -0.125 to 0.125
- expert_ids: int32 [1024, 2], P(('dp', 'expert', 'tensor')), may hold values from 0 to 7, all different within a row; in each aligned block of 32 rows (0 to 31, 32 to 63, ...) at most 9 rows name the same one
- down_weight: bfloat16 [61440, 2048], P(('expert', 'tensor')), may hold values from -0.0625 to 0.0625
- hidden: bfloat16 [4, 72, 61440], P('dp', None, ('expert', 'tensor')), may hold values from -6 to 6
- grad_output: bfloat16 [1024, 2048], P(('dp', 'expert', 'tensor')), may hold values from -4 to 4
Outputs:
- weight_grad: bfloat16 [61440, 2048], P(('expert', 'tensor', 'dp'))
- hidden_grad: bfloat16 [4, 72, 61440], P('dp', None, ('expert', 'tensor'))
- router_grad: float32 [2048, 8], replicated
- input_grad: bfloat16 [1024, 2048], P(('dp', 'expert', 'tensor'))
Inputs may be any that keep to these rules, and one draw needn't show every extreme that they name: `expert_ids`: each row names 2 different experts. Within the 32 rows of one device no expert is named more than 9 times, and some device's rows name some expert exactly 9 times.
All inputs are finite; a program needn't handle non-finite values.
Results may differ from a plain program's by a relative error of at most 0.018.
Values may be sent and summed in bfloat16 or wider, within the bound.
No kernel may reach another device: no remote copies, remote signals or barrier semaphores. Data moves between devices by JAX's collectives and lax.ppermute only.
A program may use at most 192 MiB of HBM per device.

v0:
```python
import jax
import jax.numpy as jnp
from jax import lax
from jax.sharding import PartitionSpec as P


def per_device(router_input, router_weight, expert_ids, down_weight, hidden, grad_output):
    token_rows = grad_output.shape[0]
    model_width = grad_output.shape[1]
    expert_count = router_weight.shape[1]
    choose_count = expert_ids.shape[1]
    expert_ranks = lax.axis_size("expert")
    tensor_ranks = lax.axis_size("tensor")
    sources = expert_ranks * tensor_ranks
    spread = sources // expert_count
    capacity = hidden.shape[1] // sources
    full_input = lax.all_to_all(router_input, "tensor", split_axis=0, concat_axis=1, tiled=True)
    logits = jnp.dot(full_input, router_weight, preferred_element_type=jnp.float32)
    labels = jnp.arange(expert_count, dtype=jnp.int32)
    onehot_int = (expert_ids[:, :, None] == labels).astype(jnp.int32)
    onehot = onehot_int.astype(jnp.float32)
    picked = jnp.sum(onehot * logits[:, None, :], axis=2)
    first_gate = jax.nn.sigmoid(picked[:, 0] - picked[:, 1])
    second_gate = jax.nn.sigmoid(picked[:, 1] - picked[:, 0])
    gate_values = jnp.stack([first_gate, second_gate], axis=1)
    gate_low = gate_values.astype(jnp.bfloat16)
    flat_hits = onehot_int.reshape(token_rows * choose_count, expert_count)
    before = jnp.cumsum(flat_hits, axis=0) - flat_hits
    slot_pos = jnp.sum(before * flat_hits, axis=1).reshape(token_rows, choose_count)
    slot_ids = jnp.arange(capacity, dtype=jnp.int32)
    dispatch_table = onehot[:, :, :, None] * (slot_pos[:, :, None, None] == slot_ids).astype(
        jnp.float32
    )
    slot_table = jnp.sum(dispatch_table, axis=1).astype(jnp.bfloat16)
    packed_grad = jnp.einsum(
        "rec,rd->ecd", slot_table, grad_output, preferred_element_type=jnp.float32
    ).astype(jnp.bfloat16)
    packed_gate = jnp.einsum("rkec,rk->ec", dispatch_table, gate_low.astype(jnp.float32)).astype(
        jnp.bfloat16
    )
    send_grad = jnp.repeat(packed_grad, spread, axis=0)
    send_gate = jnp.repeat(packed_gate, spread, axis=0)
    recv_grad, recv_gate = (
        lax.all_to_all(send_grad, ("expert", "tensor"), split_axis=0, concat_axis=0, tiled=True),
        lax.all_to_all(send_gate, ("expert", "tensor"), split_axis=0, concat_axis=0, tiled=True),
    )
    recv_grad = recv_grad.reshape(sources * capacity, model_width)
    recv_gate = recv_gate.reshape(sources * capacity).astype(jnp.float32)
    hidden_rows = hidden[0]
    gated_grad = (recv_gate[:, None] * recv_grad.astype(jnp.float32)).astype(jnp.bfloat16)
    expert_image = lax.dot_general(
        recv_grad, down_weight, (((1,), (1,)), ((), ())), preferred_element_type=jnp.float32
    )
    hidden_part = (recv_gate[:, None] * expert_image).astype(jnp.bfloat16)
    gate_partial = jnp.sum(hidden_rows.astype(jnp.float32) * expert_image, axis=1).reshape(
        sources, capacity
    )
    returned = lax.all_to_all(
        gate_partial, ("expert", "tensor"), split_axis=0, concat_axis=0, tiled=True
    )
    expert_sums = jnp.sum(returned.reshape(expert_count, spread, capacity), axis=1)
    gate_grad = jnp.einsum("rkec,ec->rk", dispatch_table, expert_sums)
    mixed_term = jnp.sum(gate_values * gate_grad, axis=1, keepdims=True)
    logit_part = gate_values * (gate_grad - mixed_term)
    logit_grad = jnp.sum(onehot * logit_part[:, :, None], axis=1)
    input_grad = jnp.dot(
        logit_grad, router_weight.astype(jnp.float32).T, precision=lax.Precision.HIGHEST
    ).astype(jnp.bfloat16)
    router_local = jnp.dot(
        full_input.astype(jnp.float32).T, logit_grad, precision=lax.Precision.HIGHEST
    )
    router_grad = lax.psum(router_local, ("dp", "expert", "tensor"))
    weight_sum = lax.psum_scatter(
        lax.dot_general(
            hidden_rows, gated_grad, (((0,), (0,)), ((), ())), preferred_element_type=jnp.float32
        ).astype(jnp.bfloat16),
        "dp",
        scatter_dimension=0,
        tiled=True,
    )
    return (weight_sum, hidden_part[None], router_grad, input_grad)


def solution(mesh):
    return jax.shard_map(
        per_device,
        mesh=mesh,
        in_specs=(
            P(("dp", "expert"), "tensor"),
            P(),
            P(("dp", "expert", "tensor"), None),
            P(("expert", "tensor"), None),
            P("dp", None, ("expert", "tensor")),
            P(("dp", "expert", "tensor"), None),
        ),
        out_specs=(
            P(("expert", "tensor", "dp"), None),
            P("dp", None, ("expert", "tensor")),
            P(),
            P(("dp", "expert", "tensor"), None),
        ),
        check_vma=False,
    )
```

profile of v0, /device:TPU:0, one launch (start us, length us, event | category | flops | bytes accessed | tf_op | source)
XLA Modules:
  0.0 359.2 jit_solution(10456292851233868904)
XLA Ops:
  8.0 0.0 copy-start
  8.0 0.0 copy-start.2
  8.0 4.4 %all-to-all-start = ((bf16[2,32,1024]{2,1,0:T(8,128)(2,1)}), bf16[2,32,1024]{2,1,0:T(8,128)(2,1)S(1)}, u32[]{:S(2)}, u32[]{:S(2)}) async-start(bf16[2,32,1024]{2,1,0:T(8,128)(2,1)} %bitcast.52), calls=%async_computation | async-start | bytes 262144 | tf_op jit(solution)/shard_map/all_to_all | solution.py:17
  12.4 0.8 copy.28
  13.2 0.7 convert_convert_fusion
  13.8 0.1 eq.49
  13.9 0.1 fusion.10
  14.0 0.1 reduce_window_sum.11
  14.1 0.2 select_reduce_fusion
  14.3 0.1 eq.53
  14.4 0.1 copy.29
  14.5 2.4 all-to-all-done
  17.0 0.9 fusion.15
  17.9 0.7 multiply_reduce_fusion.3
  18.6 0.2 fusion.2
  18.8 0.1 copy.37
  18.9 0.6 copy.31
  19.5 5.4 %all-to-all-start.1 = ((bf16[8,1,9]{2,1,0:T(2,128)(2,1)}), bf16[8,1,9]{2,1,0:T(2,128)(2,1)S(1)}, u32[]{:S(2)}, u32[]{:S(2)}) async-start(bf16[8,1,9]{2,1,0:T(2,128)(2,1)} %copy.31), calls=%async_computation.1 | async-start | bytes 8192 | tf_op jit(solution)/shard_map/all_to_all | solution.py:45
  24.9 1.1 convolution_convert_fusion
  26.0 5.3 %all-to-all-done.1 = bf16[8,1,9]{2,1,0:T(2,128)(2,1)S(1)} async-done(((bf16[8,1,9]{2,1,0:T(2,128)(2,1)}), bf16[8,1,9]{2,1,0:T(2,128)(2,1)S(1)}, u32[]{:S(2)}, u32[]{:S(2)}) %all-to-all-start.1) | async-done | bytes 176 | tf_op jit(solution)/shard_map/all_to_all | solution.py:45
  31.3 3.5 all-to-all-start.2
  34.9 0.1 reshape.65
  34.9 12.0 %all-to-all-done.2 = bf16[8,9,2048]{2,1,0:T(8,128)(2,1)S(1)} async-done(((bf16[8,9,2048]{2,1,0:T(8,128)(2,1)}), bf16[8,9,2048]{2,1,0:T(8,128)(2,1)S(1)}, u32[]{:S(2)}, u32[]{:S(2)}) %all-to-all-start.2) | async-done | bytes 294944 | tf_op jit(solution)/shard_map/all_to_all | solution.py:44
  47.0 0.1 reshape.63
  47.1 0.0 copy-done.2
  47.1 0.0 copy-start.4
  47.1 15.5 %multiply_reduce_fusion = (f32[72]{0:T(128)S(1)}, bf16[1,72,7680]{2,1,0:T(8,128)(2,1)}) fusion(bf16[1,72,7680]{2,1,0:T(8,128)(2,1)S(1)} %copy-done.2, f32[72]{0:T(128)S(1)} %reshape.65, bf16[72,2048]{1,0:T(8,128)(2,1)S(1)} %reshape.63, bf16[7680,2048]{1,0:T(8,128)(2,1)} %param.9), kind=kOutput, calls=%fused_computation.4 | convolution fusion | flops 2267688960 | bytes 33964608 | tf_op jit(solution)/shard_map/dot_general | solution.py:51
  62.6 0.7 all_to_all.36
  63.3 3.7 %all-to-all-start.3 = ((f32[8,1,9]{2,1,0:T(1,128)}), f32[8,1,9]{2,1,0:T(1,128)S(1)}, u32[]{:S(2)}, u32[]{:S(2)}) async-start(f32[8,1,9]{2,1,0:T(1,128)} %bitcast.12), calls=%async_computation.3 | async-start | bytes 8192 | tf_op jit(solution)/shard_map/all_to_all | solution.py:58
  67.0 0.0 all-reduce.2.cloned.1.call-start
  67.0 0.2 multiply_convert_fusion.1
  67.2 0.1 convert_element_type.93
  67.3 6.1 %all-to-all-done.3 = f32[8,1,9]{2,1,0:T(1,128)S(1)} async-done(((f32[8,1,9]{2,1,0:T(1,128)}), f32[8,1,9]{2,1,0:T(1,128)S(1)}, u32[]{:S(2)}, u32[]{:S(2)}) %all-to-all-start.3) | async-done | bytes 320 | tf_op jit(solution)/shard_map/all_to_all | solution.py:58
  73.4 0.1 copy.45
  73.5 0.1 fusion.6
  73.6 0.0 copy-done.4
  73.6 0.8 convolution_bitcast_fusion
  74.4 0.0 all-reduce.2.cloned.1.call-update
  74.5 0.0 reduce-scatter.4.cloned.1.call-start
  74.5 13.9 %convert_bitcast_fusion = bf16[7680,2048]{0,1:T(8,128)(2,1)} fusion(bf16[72,2048]{1,0:T(8,128)(2,1)S(1)} %convert_element_type.93, bf16[1,72,7680]{2,1,0:T(8,128)(2,1)S(1)} %copy-done.2), kind=kOutput, calls=%fused_computation | convolution fusion | flops 2280652800 | bytes 32858112 | tf_op jit(solution)/shard_map/dot_general | solution.py:74
  88.4 40.7 %copy.43 = bf16[7680,2048]{1,0:T(8,128)(2,1)} copy(bf16[7680,2048]{0,1:T(8,128)(2,1)} %convert_bitcast_fusion) | data formatting | bytes 62914560
  129.0 0.0 reduce-scatter.4.cloned.1.call-update
  129.1 0.7 copy-done.3
  129.8 1.0 convolution_convert_fusion.1
  130.8 159.6 %all-reduce.2.cloned.1.call-done = f32[2048,8]{0,1:T(8,128)} async-done(((f32[2048,8]{0,1:T(8,128)}), f32[2048,8]{0,1:T(8,128)}) %all-reduce.2.cloned.1.call-update) | async-done | bytes 65552 | tf_op jit(solution)/shard_map/psum | solution.py:72
  290.4 59.9 %reduce-scatter.4.cloned.1.call-done = bf16[1920,2048]{1,0:T(8,128)(2,1)} async-done(((bf16[7680,2048]{1,0:T(8,128)(2,1)}), bf16[1920,2048]{1,0:T(8,128)(2,1)}) %reduce-scatter.4.cloned.1.call-update) | async-done | bytes 7864336
  350.2 1.5 copy.55
  351.7 0.0 copy-done.1
  (13 shorter events, 0.1 us)
Async XLA Ops:
  8.0 16.9 %copy-start = (bf16[32,2048]{1,0:T(8,128)(2,1)S(1)}, bf16[32,2048]{1,0:T(8,128)(2,1)}, u32[]{:S(2)}) copy-start(bf16[32,2048]{1,0:T(8,128)(2,1)} %param.11) | copy-start | bytes 393220
  8.0 39.1 %copy-start.2 = (bf16[1,72,7680]{2,1,0:T(8,128)(2,1)S(1)}, bf16[1,72,7680]{2,1,0:T(8,128)(2,1)}, u32[]{:S(2)}) copy-start(bf16[1,72,7680]{2,1,0:T(8,128)(2,1)} %param.10) | copy-start | bytes 3317764
  8.0 8.9 %all-to-all-start = ((bf16[2,32,1024]{2,1,0:T(8,128)(2,1)}), bf16[2,32,1024]{2,1,0:T(8,128)(2,1)S(1)}, u32[]{:S(2)}, u32[]{:S(2)}) async-start(bf16[2,32,1024]{2,1,0:T(8,128)(2,1)} %bitcast.52), calls=%async_computation | async-start | bytes 262144 | tf_op jit(solution)/shard_map/all_to_all | solution.py:17
  19.5 11.8 %all-to-all-start.1 = ((bf16[8,1,9]{2,1,0:T(2,128)(2,1)}), bf16[8,1,9]{2,1,0:T(2,128)(2,1)S(1)}, u32[]{:S(2)}, u32[]{:S(2)}) async-start(bf16[8,1,9]{2,1,0:T(2,128)(2,1)} %copy.31), calls=%async_computation.1 | async-start | bytes 8192 | tf_op jit(solution)/shard_map/all_to_all | solution.py:45
  31.3 15.6 %all-to-all-start.2 = ((bf16[8,9,2048]{2,1,0:T(8,128)(2,1)}), bf16[8,9,2048]{2,1,0:T(8,128)(2,1)S(1)}, u32[]{:S(2)}, u32[]{:S(2)}) async-start(bf16[8,9,2048]{2,1,0:T(8,128)(2,1)} %convolution_convert_fusion), calls=%async_computation.2 | async-start | bytes 1048576 | tf_op jit(solution)/shard_map/all_to_all | solution.py:44
  47.1 26.5 %copy-start.4 = (s32[32,2]{0,1:T(2,128)S(1)}, s32[32,2]{0,1:T(2,128)}, u32[]{:S(2)}) copy-start(s32[32,2]{0,1:T(2,128)} %param.8) | copy-start | bytes 772
  63.3 10.1 %all-to-all-start.3 = ((f32[8,1,9]{2,1,0:T(1,128)}), f32[8,1,9]{2,1,0:T(1,128)S(1)}, u32[]{:S(2)}, u32[]{:S(2)}) async-start(f32[8,1,9]{2,1,0:T(1,128)} %bitcast.12), calls=%async_computation.3 | async-start | bytes 8192 | tf_op jit(solution)/shard_map/all_to_all | solution.py:58
  67.0 223.4 %all-reduce.2.cloned.1.call-start = ((), (), s32[]{:S(2)}) async-start(), calls=%async_computation.5 | async-start | bytes 131072 | tf_op jit(solution)/shard_map/psum | solution.py:72
  74.5 275.8 %reduce-scatter.4.cloned.1.call-start = ((), (), s32[]{:S(2)}) async-start(), calls=%async_computation.6 | async-start | bytes 39321600
  129.0 0.8 copy-start.3
  129.8 221.9 %copy-start.1 = (bf16[32,2048]{1,0:T(8,128)(2,1)S(1)}, bf16[32,2048]{1,0:T(8,128)(2,1)}, u32[]{:S(2)}) copy-start(bf16[32,2048]{1,0:T(8,128)(2,1)} %param.11) | copy-start | bytes 393220
Sparse Core Ops, SparseCore 0:
  74.6 215.7 all-reduce.1
Sparse Core Ops, SparseCore 1:
  129.2 221.0 reduce-scatter.3
where the time goes:
time: 361 us; the launch traced here: 359 us
  waiting for transfers between devices  245 us (68%)
  local copies, waits for them, and re-layouts  45.8 us (13%)
  matrix products  33.3 us (9%)
  starting transfers between devices  17 us (5%)
  between operations  15.6 us (4%)
    psum x1, waiting for transfers between devices, per_device(): router_grad = lax.psum(router_local, ('dp', 'expert', 'tensor'))  160 us
    unnamed x3, waiting for transfers between devices  59.9 us
    unnamed x14, local copies, waits for them, and re-layouts  43.7 us
    dot_general x1, matrix products, per_device(): lax.dot_general(recv_grad, down_weight, (((1,), (1,)), ((), ())), preferr...  15.5 us
    dot_general x1, matrix products, per_device(): lax.dot_general(hidden_rows, gated_grad, (((0,), (0,)), ((), ())), prefer...  13.9 us
    all_to_all x1, waiting for transfers between devices, per_device(): lax.all_to_all(send_grad, ('expert', 'tensor'), split_axis=0, concat_axis...  12 us
  transfers between devices with their start and end apart: 6, of which 6 were waited for; matrix products, arithmetic and copies ran while one was open for 16% of the time, Pallas kernels for 0%

commit v1 on v0

--- a/solution.py
+++ b/solution.py
@@ -2,6 +2,7 @@
 import jax.numpy as jnp
 from jax import lax
 from jax.sharding import PartitionSpec as P
+from jax.lax import psum
 
 
 def per_device(router_input, router_weight, expert_ids, down_weight, hidden, grad_output):
@@ -69,7 +70,9 @@
     router_local = jnp.dot(
         full_input.astype(jnp.float32).T, logit_grad, precision=lax.Precision.HIGHEST
     )
-    router_grad = lax.psum(router_local, ("dp", "expert", "tensor"))
+    router_grad = router_local
+    for jj in ("dp", ("expert", "tensor")):
+        router_grad = psum(router_grad, jj)
     weight_sum = lax.psum_scatter(
         lax.dot_general(
             hidden_rows, gated_grad, (((0,), (0,)), ((), ())), preferred_element_type=jnp.float32

time: 361 us -> 411 us (1.14)
  waiting for transfers between devices: 245 us -> 292 us
  blocking collectives: 0 us -> 9.96 us
    unnamed x3 -> x4, waiting for transfers between devices: 59.9 us -> 227 us
    psum x1 -> x2, waiting for transfers between devices: 160 us -> 45 us  [per_device(): router_grad = psum(router_grad, jj)]
    all_to_all x0 -> x1, blocking collectives: none -> 9.96 us  [per_device(): lax.all_to_all(gate_partial, ('expert', 'tensor'), split_axis=0, concat_a...]
    all_to_all x1 -> x0, waiting for transfers between devices: 6.07 us -> none  [per_device(): lax.all_to_all(gate_partial, ('expert', 'tensor'), split_axis=0, concat_a...]
  transfers between devices with their start and end apart: 6 -> 6, of which waited for: 6 -> 6; matrix products, arithmetic and copies ran while one was open for 16% -> 14% of each run, Pallas kernels for 0% -> 0%
where the time goes in v1:
time: 411 us; the launch traced here: 410 us
  waiting for transfers between devices  292 us (71%)
  local copies, waits for them, and re-layouts  45.3 us (11%)
  matrix products  33.2 us (8%)
  between operations  13.9 us (3%)
  starting transfers between devices  13.4 us (3%)
  blocking collectives  9.96 us (2%)
    unnamed x4, waiting for transfers between devices  227 us
    psum x2, waiting for transfers between devices, per_device(): router_grad = psum(router_grad, jj)  45 us
    unnamed x14, local copies, waits for them, and re-layouts  43.8 us
    dot_general x1, matrix products, per_device(): lax.dot_general(recv_grad, down_weight, (((1,), (1,)), ((), ())), preferr...  15.5 us
    dot_general x1, matrix products, per_device(): lax.dot_general(hidden_rows, gated_grad, (((0,), (0,)), ((), ())), prefer...  13.8 us
    all_to_all x1, waiting for transfers between devices, per_device(): lax.all_to_all(send_grad, ('expert', 'tensor'), split_axis=0, concat_axis...  12 us
    all_to_all x1, blocking collectives, per_device(): lax.all_to_all(gate_partial, ('expert', 'tensor'), split_axis=0, concat_a...  9.96 us
  transfers between devices with their start and end apart: 6, of which 6 were waited for; matrix products, arithmetic and copies ran while one was open for 14% of the time, Pallas kernels for 0%

profile of v1, /device:TPU:0, one launch (start us, length us, event | category | flops | bytes accessed | tf_op | source)
XLA Modules:
  0.0 409.6 jit_solution(14349591939113221509)
XLA Ops:
  7.2 0.0 copy-start
  7.2 0.0 copy-start.2
  7.2 4.4 %all-to-all-start = ((bf16[2,32,1024]{2,1,0:T(8,128)(2,1)}), bf16[2,32,1024]{2,1,0:T(8,128)(2,1)S(1)}, u32[]{:S(2)}, u32[]{:S(2)}) async-start(bf16[2,32,1024]{2,1,0:T(8,128)(2,1)} %bitcast.52), calls=%async_computation | async-start | bytes 262144 | tf_op jit(solution)/shard_map/all_to_all | solution.py:18
  11.6 0.8 copy.28
  12.3 0.7 convert_convert_fusion
  13.0 0.1 eq.49
  13.1 0.1 fusion.10
  13.2 0.1 reduce_window_sum.11
  13.3 0.2 select_reduce_fusion
  13.5 0.1 eq.53
  13.6 0.1 copy.29
  13.7 2.4 all-to-all-done
  16.1 0.9 fusion.15
  17.0 0.7 multiply_reduce_fusion.3
  17.8 0.2 fusion.2
  18.0 0.1 copy.37
  18.1 0.6 copy.31
  18.7 5.4 %all-to-all-start.1 = ((bf16[8,1,9]{2,1,0:T(2,128)(2,1)}), bf16[8,1,9]{2,1,0:T(2,128)(2,1)S(1)}, u32[]{:S(2)}, u32[]{:S(2)}) async-start(bf16[8,1,9]{2,1,0:T(2,128)(2,1)} %copy.31), calls=%async_computation.1 | async-start | bytes 8192 | tf_op jit(solution)/shard_map/all_to_all | solution.py:46
  24.1 0.0 copy-done
  24.1 1.1 convolution_convert_fusion
  25.2 5.3 %all-to-all-done.1 = bf16[8,1,9]{2,1,0:T(2,128)(2,1)S(1)} async-done(((bf16[8,1,9]{2,1,0:T(2,128)(2,1)}), bf16[8,1,9]{2,1,0:T(2,128)(2,1)S(1)}, u32[]{:S(2)}, u32[]{:S(2)}) %all-to-all-start.1) | async-done | bytes 176 | tf_op jit(solution)/shard_map/all_to_all | solution.py:46
  30.5 3.5 all-to-all-start.2
  34.0 0.0 all-reduce.3.cloned.1.call-start
  34.1 0.1 reshape.65
  34.1 12.0 %all-to-all-done.2 = bf16[8,9,2048]{2,1,0:T(8,128)(2,1)S(1)} async-done(((bf16[8,9,2048]{2,1,0:T(8,128)(2,1)}), bf16[8,9,2048]{2,1,0:T(8,128)(2,1)S(1)}, u32[]{:S(2)}, u32[]{:S(2)}) %all-to-all-start.2) | async-done | bytes 294944 | tf_op jit(solution)/shard_map/all_to_all | solution.py:45
  46.1 0.1 reshape.63
  46.3 0.0 copy-start.4
  46.3 15.5 %multiply_reduce_fusion = (f32[72]{0:T(128)S(1)}, bf16[1,72,7680]{2,1,0:T(8,128)(2,1)}) fusion(bf16[1,72,7680]{2,1,0:T(8,128)(2,1)S(1)} %copy-done.2, f32[72]{0:T(128)S(1)} %reshape.65, bf16[72,2048]{1,0:T(8,128)(2,1)S(1)} %reshape.63, bf16[7680,2048]{1,0:T(8,128)(2,1)} %param.9), kind=kOutput, calls=%fused_computation.4 | convolution fusion | flops 2267688960 | bytes 33964608 | tf_op jit(solution)/shard_map/dot_general | solution.py:52
  61.8 0.1 all_to_all.36
  61.9 10.0 %all_to_all.42 = f32[8,1,9]{2,1,0:T(1,128)S(1)} all-to-all(f32[8,1,9]{2,1,0:T(1,128)S(1)} %bitcast.54), channel_id=1, replica_groups=mesh['dp'=4,'expert'=4,'tensor'=2] {'expert','tensor'}, dimensions={0} | all-to-all | bytes 576 | tf_op jit(solution)/shard_map/all_to_all | solution.py:59
  71.8 0.1 copy.45
  71.9 0.1 fusion.6
  72.1 0.8 convolution_bitcast_fusion
  72.9 0.0 all-reduce.3.cloned.1.call-update
  72.9 0.0 all-reduce.5.cloned.1.call-start
  72.9 0.2 multiply_convert_fusion.1
  73.1 0.1 convert_element_type.93
  73.2 28.6 %all-reduce.3.cloned.1.call-done = f32[2048,8]{0,1:T(8,128)} async-done(((f32[2048,8]{0,1:T(8,128)}), f32[2048,8]{0,1:T(8,128)}) %all-reduce.3.cloned.1.call-update) | async-done | bytes 65552 | tf_op jit(solution)/shard_map/psum | solution.py:75
  101.9 0.0 all-reduce.5.cloned.1.call-update
  101.9 0.0 reduce-scatter.4.cloned.1.call-start
  101.9 13.8 %convert_bitcast_fusion = bf16[7680,2048]{0,1:T(8,128)(2,1)} fusion(bf16[72,2048]{1,0:T(8,128)(2,1)S(1)} %convert_element_type.93, bf16[1,72,7680]{2,1,0:T(8,128)(2,1)S(1)} %copy-done.2), kind=kOutput, calls=%fused_computation | convolution fusion | flops 2280652800 | bytes 32858112 | tf_op jit(solution)/shard_map/dot_general | solution.py:77
  115.7 40.7 %copy.43 = bf16[7680,2048]{1,0:T(8,128)(2,1)} copy(bf16[7680,2048]{0,1:T(8,128)(2,1)} %convert_bitcast_fusion) | data formatting | bytes 62914560
  156.5 0.0 reduce-scatter.4.cloned.1.call-update
  156.5 0.7 copy-done.3
  157.2 1.0 convolution_convert_fusion.1
  158.2 16.4 %all-reduce.5.cloned.1.call-done = f32[2048,8]{0,1:T(8,128)} async-done(((f32[2048,8]{0,1:T(8,128)}), f32[2048,8]{0,1:T(8,128)}) %all-reduce.5.cloned.1.call-update) | async-done | bytes 65552 | tf_op jit(solution)/shard_map/psum | solution.py:75
  174.6 227.0 %reduce-scatter.4.cloned.1.call-done = bf16[1920,2048]{1,0:T(8,128)(2,1)} async-done(((bf16[7680,2048]{1,0:T(8,128)(2,1)}), bf16[1920,2048]{1,0:T(8,128)(2,1)}) %reduce-scatter.4.cloned.1.call-update) | async-done | bytes 7864336
  401.6 1.5 copy.56
  (15 shorter events, 0.1 us)
Async XLA Ops:
  7.2 16.9 %copy-start = (bf16[32,2048]{1,0:T(8,128)(2,1)S(1)}, bf16[32,2048]{1,0:T(8,128)(2,1)}, u32[]{:S(2)}) copy-start(bf16[32,2048]{1,0:T(8,128)(2,1)} %param.11) | copy-start | bytes 393220
  7.2 39.1 %copy-start.2 = (bf16[1,72,7680]{2,1,0:T(8,128)(2,1)S(1)}, bf16[1,72,7680]{2,1,0:T(8,128)(2,1)}, u32[]{:S(2)}) copy-start(bf16[1,72,7680]{2,1,0:T(8,128)(2,1)} %param.10) | copy-start | bytes 3317764
  7.2 8.9 %all-to-all-start = ((bf16[2,32,1024]{2,1,0:T(8,128)(2,1)}), bf16[2,32,1024]{2,1,0:T(8,128)(2,1)S(1)}, u32[]{:S(2)}, u32[]{:S(2)}) async-start(bf16[2,32,1024]{2,1,0:T(8,128)(2,1)} %bitcast.52), calls=%async_computation | async-start | bytes 262144 | tf_op jit(solution)/shard_map/all_to_all | solution.py:18
  18.7 11.8 %all-to-all-start.1 = ((bf16[8,1,9]{2,1,0:T(2,128)(2,1)}), bf16[8,1,9]{2,1,0:T(2,128)(2,1)S(1)}, u32[]{:S(2)}, u32[]{:S(2)}) async-start(bf16[8,1,9]{2,1,0:T(2,128)(2,1)} %copy.31), calls=%async_computation.1 | async-start | bytes 8192 | tf_op jit(solution)/shard_map/all_to_all | solution.py:46
  30.5 15.6 %all-to-all-start.2 = ((bf16[8,9,2048]{2,1,0:T(8,128)(2,1)}), bf16[8,9,2048]{2,1,0:T(8,128)(2,1)S(1)}, u32[]{:S(2)}, u32[]{:S(2)}) async-start(bf16[8,9,2048]{2,1,0:T(8,128)(2,1)} %convolution_convert_fusion), calls=%async_computation.2 | async-start | bytes 1048576 | tf_op jit(solution)/shard_map/all_to_all | solution.py:45
  34.0 67.9 %all-reduce.3.cloned.1.call-start = ((), (), s32[]{:S(2)}) async-start(), calls=%async_computation.5 | async-start | bytes 131072 | tf_op jit(solution)/shard_map/psum | solution.py:75
  46.3 25.8 %copy-start.4 = (s32[32,2]{0,1:T(2,128)S(1)}, s32[32,2]{0,1:T(2,128)}, u32[]{:S(2)}) copy-start(s32[32,2]{0,1:T(2,128)} %param.8) | copy-start | bytes 772
  72.9 101.7 %all-reduce.5.cloned.1.call-start = ((), (), s32[]{:S(2)}) async-start(), calls=%async_computation.6 | async-start | bytes 131072 | tf_op jit(solution)/shard_map/psum | solution.py:75
  101.9 299.7 %reduce-scatter.4.cloned.1.call-start = ((), (), s32[]{:S(2)}) async-start(), calls=%async_computation.7 | async-start | bytes 39321600
  156.5 0.8 copy-start.3
  157.2 245.8 %copy-start.1 = (bf16[32,2048]{1,0:T(8,128)(2,1)S(1)}, bf16[32,2048]{1,0:T(8,128)(2,1)}, u32[]{:S(2)}) copy-start(bf16[32,2048]{1,0:T(8,128)(2,1)} %param.11) | copy-start | bytes 393220
Sparse Core Ops, SparseCore 0:
  73.0 28.8 all-reduce.2
  105.3 69.2 all-reduce.4
  177.7 223.7 reduce-scatter.3
